TPU v7x, 32 devices: a whole 2x2x4 slice. The times are simulated.
32 devices in a mesh: member: 4 (over y, x), lat: 8 (over z, core).
Axes of the slice: x: 2, y: 2, z: 4, core: 2. Of those that a mesh axis runs over, the one named last changes fastest.
Arguments:
- state: bfloat16 [4, 64, 720, 128], P('member', 'lat'), may hold values from -6 to 6
- conv_weight: bfloat16 [9, 128, 128], replicated, may hold values from -0.1875 to 0.1875
- legendre: bfloat16 [64, 64, 64], P('lat'), may hold values from -0.75 to 0.75
- quad_weight: float32 [64], replicated, may hold values from 0.5 to 2
- spectral_gain: float32 [2, 64, 128], replicated, may hold values from -4 to 4
- project_weight: float32 [128, 16], replicated, may hold values from -0.5 to 0.5
- target: bfloat16 [16, 64, 720], P(None, 'lat'), may hold values from -10 to 10
Outputs:
- field_grad: float32 [4, 16, 64, 720], P('member', None, 'lat')
All inputs are finite; a program needn't handle non-finite values.
Results may differ from a plain program's by a relative error of at most 0.0088.
Values may be sent and summed in bfloat16 or wider, within the bound.
A program may use at most 64 MiB of HBM per device.

v0:
```python
import jax
import jax.numpy as jnp
from jax import lax
from jax.sharding import PartitionSpec as P


def with_halo(block, sides, width):
    for axis, dim in sides:
        count = lax.axis_size(axis)
        forward = [(i, i + 1) for i in range(count - 1)]
        backward = [(target, source) for source, target in forward]
        low = lax.ppermute(
            lax.slice_in_dim(block, block.shape[dim] - width, None, axis=dim), axis, forward
        )
        high = lax.ppermute(lax.slice_in_dim(block, 0, width, axis=dim), axis, backward)
        block = jnp.concatenate([low, block, high], axis=dim)
    return block


def dft_table(nlon, modes):
    lon = jnp.arange(nlon, dtype=jnp.int32)
    wave = jnp.arange(modes, dtype=jnp.int32)
    phase = lon[:, None] * wave[None, :] % nlon
    angle = phase.astype(jnp.float32) * (2.0 * jnp.pi / nlon)
    table = jnp.concatenate([jnp.cos(angle), -jnp.sin(angle)], axis=1) / jnp.sqrt(jnp.float32(nlon))
    return table.astype(jnp.bfloat16)


def smooth(diff):
    return diff / jnp.sqrt(diff * diff + 0.25)


def local(state, conv_weight, legendre, quad_weight, spectral_gain, project_weight, target):
    field = state[0]
    lat_rows, nlon, chans = field.shape
    modes = legendre.shape[1]
    padded = with_halo(field, (("lat", 0),), 4)
    conv = jnp.zeros((lat_rows, nlon, chans), jnp.float32)
    for shift in range(9):
        conv = conv + jnp.einsum(
            "anc,cd->and",
            padded[shift : shift + lat_rows],
            conv_weight[shift],
            preferred_element_type=jnp.float32,
        )
    mixed = (field.astype(jnp.float32) + jax.nn.silu(conv)).astype(jnp.bfloat16)
    table = dft_table(nlon, modes)
    spectrum = jnp.einsum("anc,nk->akc", mixed, table, preferred_element_type=jnp.float32).astype(
        jnp.bfloat16
    )
    spectrum = spectrum.reshape(lat_rows, 2, modes, chans)
    banded = lax.all_to_all(spectrum, "lat", split_axis=2, concat_axis=0, tiled=True)
    wtable = (legendre.astype(jnp.float32) * quad_weight[None, None, :]).astype(jnp.bfloat16)
    coef = jnp.einsum("mla,armc->mlrc", wtable, banded, preferred_element_type=jnp.float32)
    gain_re = spectral_gain[0]
    gain_im = spectral_gain[1]
    real_part = coef[:, :, 0] * gain_re[None] - coef[:, :, 1] * gain_im[None]
    imag_part = coef[:, :, 0] * gain_im[None] + coef[:, :, 1] * gain_re[None]
    filtered = jnp.stack([real_part, imag_part], axis=2).astype(jnp.bfloat16)
    back = jnp.einsum(
        "mla,mlrc->armc", legendre, filtered, preferred_element_type=jnp.float32
    ).astype(jnp.bfloat16)
    rowwise = lax.all_to_all(back, "lat", split_axis=0, concat_axis=2, tiled=True)
    synth = jnp.einsum(
        "akc,nk->anc",
        rowwise.reshape(lat_rows, 2 * modes, chans),
        table,
        preferred_element_type=jnp.float32,
    )
    total = mixed.astype(jnp.float32) + synth
    projected = jnp.einsum(
        "anc,cf->fan", total, project_weight, precision=lax.Precision.HIGHEST
    ).astype(jnp.bfloat16)
    members = lax.axis_size("member")
    own = projected.astype(jnp.float32)
    pair = jnp.sum(
        smooth(
            own[None]
            - lax.all_gather(projected[None], "member", axis=0, tiled=True).astype(jnp.float32)
        ),
        axis=0,
    )
    grads = smooth(own - target.astype(jnp.float32)) - pair / (members - 1)
    return grads[None]


def solution(mesh):
    return jax.shard_map(
        local,
        mesh=mesh,
        in_specs=(
            P("member", "lat", None, None),
            P(),
            P("lat", None, None),
            P(),
            P(),
            P(),
            P(None, "lat", None),
        ),
        out_specs=P("member", None, "lat", None),
        check_vma=False,
    )
```

profile of v0, /device:TPU:0, one launch (start us, length us, event | category | flops | bytes accessed | tf_op | source)
XLA Modules:
  0.0 73.4 jit_solution(10535951291946329749)
XLA Ops:
  0.0 0.0 copy-start
  0.0 0.0 copy-start.1
  0.0 0.0 copy-start.3
  0.0 1.6 %slice_bitcast_fusion.1 = (bf16[4,720,128]{2,1,0:T(8,128)(2,1)S(1)}, bf16[4,720,128]{2,1,0:T(8,128)(2,1)S(1)}) fusion(bf16[1,8,720,128]{3,2,1,0:T(8,128)(2,1)} %param.7), kind=kLoop, calls=%fused_computation.18 | loop fusion | bytes 2949120 | tf_op jit(solution)/shard_map/slice | solution.py:13
  1.6 1.3 %collective-permute-start.1 = (bf16[4,720,128]{2,1,0:T(8,128)(2,1)S(1)}, bf16[4,720,128]{2,1,0:T(8,128)(2,1)S(1)}, u32[]{:S(2)}, u32[]{:S(2)}) collective-permute-start(bf16[4,720,128]{2,1,0:T(8,128)(2,1)S(1)} %get-tuple-element.6), channel_id=1, source_target_pairs={{1,0},{2,1},{3,2},{4,3},{5,4},{6,5},{7,6},{9,8},{10,9},{11,10},{12... | collective-permute-start | bytes 2211848 | tf_op jit(solution)/shard_map/ppermute | solution.py:15
  2.9 3.1 %collective-permute-start = (bf16[4,720,128]{2,1,0:T(8,128)(2,1)S(1)}, bf16[4,720,128]{2,1,0:T(8,128)(2,1)S(1)}, u32[]{:S(2)}, u32[]{:S(2)}) collective-permute-start(bf16[4,720,128]{2,1,0:T(8,128)(2,1)S(1)} %get-tuple-element.5), channel_id=1, source_target_pairs={{0,1},{1,2},{2,3},{3,4},{4,5},{5,6},{6,7},{8,9},{9,10},{10,11},{11... | collective-permute-start | bytes 2211848 | tf_op jit(solution)/shard_map/ppermute | solution.py:12
  6.0 1.5 %sine_negate_fusion = (f32[720,64]{1,0:T(8,128)S(1)}, f32[720,64]{1,0:T(8,128)S(1)}) fusion(), kind=kLoop, calls=%fused_computation.25 | loop fusion | flops 460800 | bytes 368640 | tf_op jit(solution)/shard_map/neg | solution.py:25
  7.5 0.2 fusion.23
  7.7 0.0 copy-done.1
  7.7 0.0 copy-done.3
  7.7 2.1 %fusion.38 = f32[8,720,128]{2,1,0:T(8,128)} fusion(bf16[9,128,128]{2,1,0:T(8,128)(2,1)S(1)} %copy-done.3, bf16[1,8,720,128]{3,2,1,0:T(8,128)(2,1)S(1)} %copy-done.1), kind=kOutput, calls=%fused_computation.52 | convolution fusion | flops 188743680 | bytes 4456448 | tf_op jit(solution)/shard_map/anc,cd->and/dot_general | solution.py:40
  9.8 0.0 collective-permute-done.1
  9.8 0.5 fusion.32
  10.4 0.5 fusion.34
  10.9 0.5 fusion.36
  11.4 0.0 collective-permute-done
  11.4 0.5 fusion.40
  11.9 0.5 fusion.42
  12.5 2.2 %fusion.44 = f32[8,720,128]{2,1,0:T(8,128)} fusion(bf16[9,128,128]{2,1,0:T(8,128)(2,1)S(1)} %copy-done.3, bf16[8,720,128]{2,1,0:T(8,128)(2,1)S(1)} %bitcast.105, bf16[4,720,128]{2,1,0:T(8,128)(2,1)S(1)} %collective-permute-done), kind=kOutput, calls=%fused_computation.58 | convolution fusion | flops 193167360 | bytes 5193728 | tf_op jit(solution)/shard_map/anc,cd->and/dot_general | solution.py:40
  14.7 2.1 %fusion.46 = f32[8,720,128]{2,1,0:T(8,128)} fusion(bf16[9,128,128]{2,1,0:T(8,128)(2,1)S(1)} %copy-done.3, bf16[8,720,128]{2,1,0:T(8,128)(2,1)S(1)} %bitcast.106, bf16[4,720,128]{2,1,0:T(8,128)(2,1)S(1)} %collective-permute-done), kind=kOutput, calls=%fused_computation.60 | convolution fusion | flops 193167360 | bytes 5193728 | tf_op jit(solution)/shard_map/anc,cd->and/dot_general | solution.py:40
  16.8 4.7 %add_convert_fusion = bf16[8,720,128]{2,1,0:T(8,128)(2,1)S(1)} fusion(f32[8,720,128]{2,1,0:T(8,128)S(1)} %fusion.32, f32[8,720,128]{2,1,0:T(8,128)S(1)} %fusion.34, f32[8,720,128]{2,1,0:T(8,128)S(1)} %fusion.36, f32[8,720,128]{2,1,0:T(8,128)} %fusion.38, f32[8,720,128]{2,1,0:T(8,128)S(1)} %fusion.40, f32[8,720,128]{2,1,0:T(8,128)S(1)} %fusion.42, ...), kind=kOutput, calls=%fused_computation.3 | convolution fusion | flops 204226560 | bytes 28786688 | tf_op jit(solution)/shard_map/anc,cd->and/dot_general | solution.py:40
  21.5 0.0 copy-start.5
  21.5 0.0 copy-start.2
  21.5 0.0 copy-start.6
  21.5 0.4 convolution_convert_fusion.1
  21.9 1.0 %copy.23 = bf16[8,2,64,128]{3,1,0,2:T(2,128)(2,1)} copy(bf16[8,2,64,128]{3,2,1,0:T(8,128)(2,1)S(1)} %bitcast.112) | data formatting | bytes 524288 | tf_op jit(solution)/shard_map/reshape | solution.py:51
  22.9 11.2 %all-to-all-start = ((bf16[8,2,64,128]{3,1,0,2:T(2,128)(2,1)}), bf16[8,2,64,128]{3,1,0,2:T(2,128)(2,1)S(1)}, u32[]{:S(2)}, u32[]{:S(2)}) async-start(bf16[8,2,64,128]{3,1,0,2:T(2,128)(2,1)} %copy.23), calls=%async_computation | async-start | bytes 524288 | tf_op jit(solution)/shard_map/all_to_all | solution.py:52
  34.1 0.0 copy-done.5
  34.1 9.7 %all-to-all-done = bf16[8,2,64,128]{3,1,0,2:T(2,128)(2,1)S(1)} async-done(((bf16[8,2,64,128]{3,1,0,2:T(2,128)(2,1)}), bf16[8,2,64,128]{3,1,0,2:T(2,128)(2,1)S(1)}, u32[]{:S(2)}, u32[]{:S(2)}) %all-to-all-start) | async-done | bytes 262176 | tf_op jit(solution)/shard_map/all_to_all | solution.py:52
  43.8 0.0 copy-done.2
  43.8 0.0 copy-done.6
  43.8 0.2 fusion.20
  44.0 0.1 subtract_convert_fusion
  44.1 0.3 fusion.8
  44.4 0.3 copy.26
  44.7 12.1 %all_to_all.33 = bf16[64,2,8,128]{3,1,2,0:T(2,128)(2,1)S(1)} all-to-all(bf16[64,2,8,128]{3,1,2,0:T(2,128)(2,1)S(1)} %copy.26), channel_id=1, replica_groups=mesh['member'=4,'lat'=8] {'lat'}, dimensions={0} | all-to-all | bytes 524288 | tf_op jit(solution)/shard_map/all_to_all | solution.py:63
  56.8 0.1 copy.28
  56.9 0.5 fusion.61
  57.5 0.0 copy-done
  57.5 0.0 copy-start.4
  57.5 3.3 %fusion.60 = (f32[16,8,720]{2,0,1:T(8,128)S(1)}, bf16[16,8,720]{2,0,1:T(8,128)(2,1)S(1)}) fusion(f32[128,16]{0,1:T(8,128)S(1)} %copy-done, f32[720,8,128]{2,0,1:T(8,128)S(1)} %fusion.61, bf16[8,720,128]{2,1,0:T(8,128)(2,1)S(1)} %add_convert_fusion), kind=kOutput, calls=%fused_computation.76 | convolution fusion | flops 143216640 | bytes 4984832 | tf_op jit(solution)/shard_map/anc,cf->fan/dot_general | solution.py:71
  60.8 11.1 %all-gather = bf16[64,8,720]{2,0,1:T(8,128)(2,1)S(1)} all-gather(bf16[16,8,720]{2,0,1:T(8,128)(2,1)S(1)} %get-tuple-element.12), channel_id=2, replica_groups=mesh['member'=4,'lat'=8] {'member'}, dimensions={0}, use_global_device_ids=true | all-gather | bytes 921600 | tf_op jit(solution)/shard_map/all_gather | solution.py:79
  71.9 0.4 fusion.6
  72.3 0.0 copy-done.4
  72.3 0.1 subtract_bitcast_fusion
  72.5 1.0 %copy.30 = f32[1,16,8,720]{3,2,1,0:T(8,128)} copy(f32[1,16,8,720]{3,1,2,0:T(8,128)S(1)} %subtract_bitcast_fusion) | data formatting | bytes 737280 | tf_op jit(solution)/shard_map/broadcast_in_dim | solution.py:84
  (2 shorter events, 0.0 us)
Async XLA Ops:
  0.0 57.5 %copy-start = (f32[128,16]{0,1:T(8,128)S(1)}, f32[128,16]{0,1:T(8,128)}, u32[]{:S(2)}) copy-start(f32[128,16]{0,1:T(8,128)} %param.12) | copy-start | bytes 24580
  0.0 7.7 %copy-start.1 = (bf16[1,8,720,128]{3,2,1,0:T(8,128)(2,1)S(1)}, bf16[1,8,720,128]{3,2,1,0:T(8,128)(2,1)}, u32[]{:S(2)}) copy-start(bf16[1,8,720,128]{3,2,1,0:T(8,128)(2,1)} %param.7) | copy-start | bytes 4423684
  0.0 7.7 %copy-start.3 = (bf16[9,128,128]{2,1,0:T(8,128)(2,1)S(1)}, bf16[9,128,128]{2,1,0:T(8,128)(2,1)}, u32[]{:S(2)}) copy-start(bf16[9,128,128]{2,1,0:T(8,128)(2,1)} %param.8) | copy-start | bytes 884740
  1.6 8.3 %collective-permute-start.1 = (bf16[4,720,128]{2,1,0:T(8,128)(2,1)S(1)}, bf16[4,720,128]{2,1,0:T(8,128)(2,1)S(1)}, u32[]{:S(2)}, u32[]{:S(2)}) collective-permute-start(bf16[4,720,128]{2,1,0:T(8,128)(2,1)S(1)} %get-tuple-element.6), channel_id=1, source_target_pairs={{1,0},{2,1},{3,2},{4,3},{5,4},{6,5},{7,6},{9,8},{10,9},{11,10},{12... | collective-permute-start | bytes 2211848 | tf_op jit(solution)/shard_map/ppermute | solution.py:15
  2.9 8.5 %collective-permute-start = (bf16[4,720,128]{2,1,0:T(8,128)(2,1)S(1)}, bf16[4,720,128]{2,1,0:T(8,128)(2,1)S(1)}, u32[]{:S(2)}, u32[]{:S(2)}) collective-permute-start(bf16[4,720,128]{2,1,0:T(8,128)(2,1)S(1)} %get-tuple-element.5), channel_id=1, source_target_pairs={{0,1},{1,2},{2,3},{3,4},{4,5},{5,6},{6,7},{8,9},{9,10},{10,11},{11... | collective-permute-start | bytes 2211848 | tf_op jit(solution)/shard_map/ppermute | solution.py:12
  21.5 12.6 %copy-start.5 = (f32[2,64,128]{2,1,0:T(8,128)S(1)}, f32[2,64,128]{2,1,0:T(8,128)}, u32[]{:S(2)}) copy-start(f32[2,64,128]{2,1,0:T(8,128)} %param.11) | copy-start | bytes 196612
  21.5 22.3 %copy-start.2 = (bf16[8,64,64]{2,1,0:T(8,128)(2,1)S(1)}, bf16[8,64,64]{2,1,0:T(8,128)(2,1)}, u32[]{:S(2)}) copy-start(bf16[8,64,64]{2,1,0:T(8,128)(2,1)} %param.9) | copy-start | bytes 196612
  21.5 22.3 %copy-start.6 = (f32[64]{0:T(128)S(1)}, f32[64]{0:T(128)}, u32[]{:S(2)}) copy-start(f32[64]{0:T(128)} %param.10) | copy-start | bytes 772
  22.9 20.9 %all-to-all-start = ((bf16[8,2,64,128]{3,1,0,2:T(2,128)(2,1)}), bf16[8,2,64,128]{3,1,0,2:T(2,128)(2,1)S(1)}, u32[]{:S(2)}, u32[]{:S(2)}) async-start(bf16[8,2,64,128]{3,1,0,2:T(2,128)(2,1)} %copy.23), calls=%async_computation | async-start | bytes 524288 | tf_op jit(solution)/shard_map/all_to_all | solution.py:52
  57.5 14.8 %copy-start.4 = (bf16[16,8,720]{2,1,0:T(8,128)(2,1)S(1)}, bf16[16,8,720]{2,1,0:T(8,128)(2,1)}, u32[]{:S(2)}) copy-start(bf16[16,8,720]{2,1,0:T(8,128)(2,1)} %param.13) | copy-start | bytes 552964
where the time goes:
time: 73.8 us; the launch traced here: 73.4 us
  blocking collectives  23.2 us (31%)
  matrix products  18.5 us (25%)
  starting transfers between devices  15.6 us (21%)
  waiting for transfers between devices  9.7 us (13%)
  local copies, waits for them, and re-layouts  3.93 us (5%)
  other arithmetic  2.31 us (3%)
    dot_general x9, matrix products, local(): jnp.einsum('anc,cd->and', padded[shift:shift + lat_rows], conv_weight[shi...  13.7 us
    all_to_all x1, blocking collectives, local(): lax.all_to_all(back, 'lat', split_axis=0, concat_axis=2, tiled=True)  12.1 us
    all_to_all x1, starting transfers between devices, local(): lax.all_to_all(spectrum, 'lat', split_axis=2, concat_axis=0, tiled=True)  11.2 us
    all_gather x1, blocking collectives, local(): lax.all_gather(projected[None], 'member', axis=0, tiled=True)  11.1 us
    all_to_all x1, waiting for transfers between devices, local(): lax.all_to_all(spectrum, 'lat', split_axis=2, concat_axis=0, tiled=True)  9.69 us
    dot_general x1, matrix products, local(): jnp.einsum('anc,cf->fan', total, project_weight, precision=lax.Precision....  3.32 us
    ppermute x1, starting transfers between devices, with_halo(): lax.ppermute(lax.slice_in_dim(block, block.shape[dim] - width, None, axis...  3.08 us
    slice x1, local copies, waits for them, and re-layouts, with_halo(): lax.slice_in_dim(block, block.shape[dim] - width, None, axis=dim)  1.56 us
  transfers between devices with their start and end apart: 3, of which 1 were waited for; matrix products, arithmetic and copies ran while one was open for 7% of the time, Pallas kernels for 0%

commit v1 on v0

--- a/solution.py
+++ b/solution.py
@@ -35,14 +35,14 @@
     lat_rows, nlon, chans = field.shape
     modes = legendre.shape[1]
     padded = with_halo(field, (("lat", 0),), 4)
-    conv = jnp.zeros((lat_rows, nlon, chans), jnp.float32)
-    for shift in range(9):
-        conv = conv + jnp.einsum(
-            "anc,cd->and",
-            padded[shift : shift + lat_rows],
-            conv_weight[shift],
-            preferred_element_type=jnp.float32,
-        )
+    conv = lax.conv_general_dilated(
+        padded,
+        conv_weight,
+        window_strides=(1,),
+        padding="VALID",
+        dimension_numbers=("WNC", "WIO", "WNC"),
+        preferred_element_type=jnp.float32,
+    )
     mixed = (field.astype(jnp.float32) + jax.nn.silu(conv)).astype(jnp.bfloat16)
     table = dft_table(nlon, modes)
     spectrum = jnp.einsum("anc,nk->akc", mixed, table, preferred_element_type=jnp.float32).astype(
@@ -60,17 +60,20 @@
     back = jnp.einsum(
         "mla,mlrc->armc", legendre, filtered, preferred_element_type=jnp.float32
     ).astype(jnp.bfloat16)
-    rowwise = lax.all_to_all(back, "lat", split_axis=0, concat_axis=2, tiled=True)
+    high = lax.reduce_precision(project_weight, 8, 7)
+    weight = jnp.concatenate([high, project_weight - high], axis=1).astype(jnp.bfloat16)
+    fields = project_weight.shape[1]
+    both = jnp.einsum("armc,cg->armg", back, weight, preferred_element_type=jnp.float32)
+    narrow = (both[..., :fields] + both[..., fields:]).astype(jnp.bfloat16)
+    rowwise = lax.all_to_all(narrow, "lat", split_axis=0, concat_axis=2, tiled=True)
     synth = jnp.einsum(
-        "akc,nk->anc",
-        rowwise.reshape(lat_rows, 2 * modes, chans),
+        "akf,nk->fan",
+        rowwise.reshape(lat_rows, 2 * modes, fields),
         table,
         preferred_element_type=jnp.float32,
     )
-    total = mixed.astype(jnp.float32) + synth
-    projected = jnp.einsum(
-        "anc,cf->fan", total, project_weight, precision=lax.Precision.HIGHEST
-    ).astype(jnp.bfloat16)
+    direct = jnp.einsum("anc,cg->gan", mixed, weight, preferred_element_type=jnp.float32)
+    projected = (direct[:fields] + direct[fields:] + synth).astype(jnp.bfloat16)
     members = lax.axis_size("member")
     own = projected.astype(jnp.float32)
     pair = jnp.sum(

time: 73.8 us -> 62.9 us (0.85)
  matrix products: 18.5 us -> 5.96 us
  blocking collectives: 23.2 us -> 11.3 us
  waiting for transfers between devices: 9.7 us -> 17.9 us
  starting transfers between devices: 15.6 us -> 19.9 us
  local copies, waits for them, and re-layouts: 3.93 us -> 4.77 us
    dot_general x11 -> x2, matrix products: 17.6 us -> 0.92 us  [the longest x1 0.65 us: local(): jnp.einsum('anc,cg->gan', mixed, weight, preferred_element_type=jnp.float32)]
    all_to_all x1 -> x0, blocking collectives: 12.1 us -> none  [local(): lax.all_to_all(back, 'lat', split_axis=0, concat_axis=2, tiled=True)]
    all_to_all x0 -> x1, waiting for transfers between devices: none -> 5.02 us  [local(): lax.all_to_all(narrow, 'lat', split_axis=0, concat_axis=2, tiled=True)]
    conv_general_dilated x0 -> x1, matrix products: none -> 3.95 us  [local(): lax.conv_general_dilated(padded, conv_weight, window_strides=(1,), paddin...]
    all_to_all x0 -> x1, starting transfers between devices: none -> 3.34 us  [local(): lax.all_to_all(narrow, 'lat', split_axis=0, concat_axis=2, tiled=True)]
    ppermute x1, waiting for transfers between devices: 0.01 us -> 3.21 us  [with_halo(): lax.ppermute(lax.slice_in_dim(block, 0, width, axis=dim), axis, backward)]
    all_to_all x1, starting transfers between devices: 11.2 us -> 12.6 us  [local(): lax.all_to_all(spectrum, 'lat', split_axis=2, concat_axis=0, tiled=True)]
    unnamed x14 -> x16, local copies, waits for them, and re-layouts: 0.04 us -> 1.16 us
  transfers between devices with their start and end apart: 3 -> 4, of which waited for: 1 -> 3; matrix products, arithmetic and copies ran while one was open for 7% -> 4% of each run, Pallas kernels for 0% -> 0%
where the time goes in v1:
time: 62.9 us; the launch traced here: 62.5 us
  starting transfers between devices  19.9 us (32%)
  waiting for transfers between devices  17.9 us (28%)
  blocking collectives  11.3 us (18%)
  matrix products  5.96 us (9%)
  local copies, waits for them, and re-layouts  4.77 us (8%)
  other arithmetic  2.58 us (4%)
    all_to_all x1, starting transfers between devices, local(): lax.all_to_all(spectrum, 'lat', split_axis=2, concat_axis=0, tiled=True)  12.6 us
    all_gather x1, blocking collectives, local(): lax.all_gather(projected[None], 'member', axis=0, tiled=True)  11.3 us
    all_to_all x1, waiting for transfers between devices, local(): lax.all_to_all(spectrum, 'lat', split_axis=2, concat_axis=0, tiled=True)  9.67 us
    all_to_all x1, waiting for transfers between devices, local(): lax.all_to_all(narrow, 'lat', split_axis=0, concat_axis=2, tiled=True)  5.02 us
    conv_general_dilated x1, matrix products, local(): lax.conv_general_dilated(padded, conv_weight, window_strides=(1,), paddin...  3.95 us
    all_to_all x1, starting transfers between devices, local(): lax.all_to_all(narrow, 'lat', split_axis=0, concat_axis=2, tiled=True)  3.34 us
    ppermute x1, waiting for transfers between devices, with_halo(): lax.ppermute(lax.slice_in_dim(block, 0, width, axis=dim), axis, backward)  3.21 us
    ppermute x1, starting transfers between devices, with_halo(): lax.ppermute(lax.slice_in_dim(block, block.shape[dim] - width, None, axis...  2.57 us
  transfers between devices with their start and end apart: 4, of which 3 were waited for; matrix products, arithmetic and copies ran while one was open for 4% of the time, Pallas kernels for 0%

profile of v1, /device:TPU:0, one launch (start us, length us, event | category | flops | bytes accessed | tf_op | source)
XLA Modules:
  0.0 62.5 jit_solution(724473177946938790)
XLA Ops:
  0.0 0.0 copy-start
  0.0 1.5 %slice_bitcast_fusion.1 = (bf16[4,720,128]{2,1,0:T(8,128)(2,1)S(1)}, bf16[4,720,128]{2,1,0:T(8,128)(2,1)S(1)}) fusion(bf16[1,8,720,128]{3,2,1,0:T(8,128)(2,1)} %param.7), kind=kLoop, calls=%fused_computation.17 | loop fusion | bytes 2949120 | tf_op jit(solution)/shard_map/slice | solution.py:13
  1.5 0.0 copy-start.1
  1.5 2.6 %collective-permute-start = (bf16[4,720,128]{2,1,0:T(8,128)(2,1)S(1)}, bf16[4,720,128]{2,1,0:T(8,128)(2,1)S(1)}, u32[]{:S(2)}, u32[]{:S(2)}) collective-permute-start(bf16[4,720,128]{2,1,0:T(8,128)(2,1)S(1)} %get-tuple-element.7), channel_id=1, source_target_pairs={{0,1},{1,2},{2,3},{3,4},{4,5},{5,6},{6,7},{8,9},{9,10},{10,11},{11... | collective-permute-start | bytes 2211848 | tf_op jit(solution)/shard_map/ppermute | solution.py:12
  4.1 1.3 %collective-permute-start.1 = (bf16[4,720,128]{2,1,0:T(8,128)(2,1)S(1)}, bf16[4,720,128]{2,1,0:T(8,128)(2,1)S(1)}, u32[]{:S(2)}, u32[]{:S(2)}) collective-permute-start(bf16[4,720,128]{2,1,0:T(8,128)(2,1)S(1)} %get-tuple-element.8), channel_id=1, source_target_pairs={{1,0},{2,1},{3,2},{4,3},{5,4},{6,5},{7,6},{9,8},{10,9},{11,10},{12... | collective-permute-start | bytes 2211848 | tf_op jit(solution)/shard_map/ppermute | solution.py:15
  5.4 1.5 %sine_negate_fusion = (f32[720,64]{1,0:T(8,128)S(1)}, f32[720,64]{1,0:T(8,128)S(1)}) fusion(), kind=kLoop, calls=%fused_computation.29 | loop fusion | flops 460800 | bytes 368640 | tf_op jit(solution)/shard_map/neg | solution.py:25
  6.9 0.2 fusion.19
  7.1 0.0 collective-permute-done
  7.1 3.2 %collective-permute-done.1 = bf16[4,720,128]{2,1,0:T(8,128)(2,1)S(1)} collective-permute-done((bf16[4,720,128]{2,1,0:T(8,128)(2,1)S(1)}, bf16[4,720,128]{2,1,0:T(8,128)(2,1)S(1)}, u32[]{:S(2)}, u32[]{:S(2)}) %collective-permute-start.1) | collective-permute-done | bytes 737312 | tf_op jit(solution)/shard_map/ppermute | solution.py:15
  10.3 0.0 copy-done
  10.3 0.0 copy-done.1
  10.3 3.9 %add_convert_fusion = bf16[8,720,128]{2,1,0:T(8,128)(2,1)S(1)} fusion(bf16[8,720,128]{2,1,0:T(8,128)(2,1)S(1)} %bitcast.62, bf16[9,128,128]{2,1,0:T(8,128)(2,1)S(1)} %copy-done, bf16[4,720,128]{2,1,0:T(8,128)(2,1)S(1)} %collective-permute-done.1, bf16[4,720,128]{2,1,0:T(8,128)(2,1)S(1)} %collective-permute-done), kind=kOutput, calls=%fused_computation.6 | convolution fusion | flops 1706803200 | bytes 4718592 | tf_op jit(solution)/shard_map/conv_general_dilated | solution.py:38
  14.3 0.0 copy-start.5
  14.3 0.0 copy-start.4
  14.3 0.0 copy-start.2
  14.3 0.0 copy-start.6
  14.3 0.4 convolution_convert_fusion.1
  14.7 1.0 %copy.17 = bf16[8,2,64,128]{3,1,0,2:T(2,128)(2,1)} copy(bf16[8,2,64,128]{3,2,1,0:T(8,128)(2,1)S(1)} %bitcast.66) | data formatting | bytes 524288 | tf_op jit(solution)/shard_map/reshape | solution.py:51
  15.7 12.6 %all-to-all-start = ((bf16[8,2,64,128]{3,1,0,2:T(2,128)(2,1)}), bf16[8,2,64,128]{3,1,0,2:T(2,128)(2,1)S(1)}, u32[]{:S(2)}, u32[]{:S(2)}) async-start(bf16[8,2,64,128]{3,1,0,2:T(2,128)(2,1)} %copy.17), calls=%async_computation | async-start | bytes 524288 | tf_op jit(solution)/shard_map/all_to_all | solution.py:52
  28.4 0.0 copy-done.5
  28.4 0.0 copy-done.4
  28.4 9.7 %all-to-all-done = bf16[8,2,64,128]{3,1,0,2:T(2,128)(2,1)S(1)} async-done(((bf16[8,2,64,128]{3,1,0,2:T(2,128)(2,1)}), bf16[8,2,64,128]{3,1,0,2:T(2,128)(2,1)S(1)}, u32[]{:S(2)}, u32[]{:S(2)}) %all-to-all-start) | async-done | bytes 262176 | tf_op jit(solution)/shard_map/all_to_all | solution.py:52
  38.1 0.0 copy-done.2
  38.1 0.0 copy-done.6
  38.1 0.2 fusion.27
  38.3 0.1 subtract_convert_fusion
  38.4 0.3 fusion.11
  38.6 0.3 fusion.29
  38.9 0.2 fusion.14
  39.1 0.9 %reshape.22 = bf16[8,2,1024]{2,1,0:T(2,128)(2,1)} reshape(bf16[64,2,8,16]{3,2,1,0:T(8,128)(2,1)S(1)} %fusion.14) | data formatting | bytes 65536
  40.0 3.3 %all-to-all-start.1 = ((bf16[8,2,1024]{2,1,0:T(2,128)(2,1)}), bf16[8,2,1024]{2,1,0:T(2,128)(2,1)S(1)}, u32[]{:S(2)}, u32[]{:S(2)}) async-start(bf16[8,2,1024]{2,1,0:T(2,128)(2,1)} %reshape.22), calls=%async_computation.1 | async-start | bytes 65536 | tf_op jit(solution)/shard_map/all_to_all | solution.py:68
  43.4 0.7 %fusion.39 = f32[32,8,720]{2,0,1:T(8,128)S(1)} fusion(bf16[8,720,128]{2,1,0:T(8,128)(2,1)S(1)} %add_convert_fusion, bf16[128,16]{0,1:T(8,128)(2,1)S(1)} %get-tuple-element.14, bf16[128,16]{0,1:T(8,128)(2,1)S(1)} %get-tuple-element.13), kind=kOutput, calls=%fused_computation.57 | convolution fusion | flops 47202304 | bytes 2220032 | tf_op jit(solution)/shard_map/anc,cg->gan/dot_general | solution.py:75
  44.0 5.0 %all-to-all-done.1 = bf16[8,2,1024]{2,1,0:T(2,128)(2,1)S(1)} async-done(((bf16[8,2,1024]{2,1,0:T(2,128)(2,1)}), bf16[8,2,1024]{2,1,0:T(2,128)(2,1)S(1)}, u32[]{:S(2)}, u32[]{:S(2)}) %all-to-all-start.1) | async-done | bytes 32800 | tf_op jit(solution)/shard_map/all_to_all | solution.py:68
  49.0 0.2 reshape.23
  49.3 0.1 copy.21
  49.3 0.1 copy.22
  49.5 0.2 fusion.47
  49.7 0.1 fusion.45
  49.8 0.0 copy-start.3
  49.8 11.3 %all-gather = bf16[64,8,720]{2,0,1:T(8,128)(2,1)S(1)} all-gather(bf16[16,8,720]{2,0,1:T(8,128)(2,1)S(1)} %get-tuple-element.6), channel_id=2, replica_groups=mesh['member'=4,'lat'=8] {'member'}, dimensions={0}, use_global_device_ids=true | all-gather | bytes 921600 | tf_op jit(solution)/shard_map/all_gather | solution.py:82
  61.0 0.4 fusion.10
  61.4 0.0 copy-done.3
  61.4 0.1 subtract_bitcast_fusion
  61.6 1.0 %copy.24 = f32[1,16,8,720]{3,2,1,0:T(8,128)} copy(f32[1,16,8,720]{3,1,2,0:T(8,128)S(1)} %subtract_bitcast_fusion) | data formatting | bytes 737280 | tf_op jit(solution)/shard_map/broadcast_in_dim | solution.py:87
  (2 shorter events, 0.0 us)
Async XLA Ops:
  0.0 10.3 %copy-start = (bf16[9,128,128]{2,1,0:T(8,128)(2,1)S(1)}, bf16[9,128,128]{2,1,0:T(8,128)(2,1)}, u32[]{:S(2)}) copy-start(bf16[9,128,128]{2,1,0:T(8,128)(2,1)} %param.8) | copy-start | bytes 884740
  1.5 8.8 %copy-start.1 = (bf16[1,8,720,128]{3,2,1,0:T(8,128)(2,1)S(1)}, bf16[1,8,720,128]{3,2,1,0:T(8,128)(2,1)}, u32[]{:S(2)}) copy-start(bf16[1,8,720,128]{3,2,1,0:T(8,128)(2,1)} %param.7) | copy-start | bytes 4423684
  1.5 5.6 %collective-permute-start = (bf16[4,720,128]{2,1,0:T(8,128)(2,1)S(1)}, bf16[4,720,128]{2,1,0:T(8,128)(2,1)S(1)}, u32[]{:S(2)}, u32[]{:S(2)}) collective-permute-start(bf16[4,720,128]{2,1,0:T(8,128)(2,1)S(1)} %get-tuple-element.7), channel_id=1, source_target_pairs={{0,1},{1,2},{2,3},{3,4},{4,5},{5,6},{6,7},{8,9},{9,10},{10,11},{11... | collective-permute-start | bytes 2211848 | tf_op jit(solution)/shard_map/ppermute | solution.py:12
  4.1 6.2 %collective-permute-start.1 = (bf16[4,720,128]{2,1,0:T(8,128)(2,1)S(1)}, bf16[4,720,128]{2,1,0:T(8,128)(2,1)S(1)}, u32[]{:S(2)}, u32[]{:S(2)}) collective-permute-start(bf16[4,720,128]{2,1,0:T(8,128)(2,1)S(1)} %get-tuple-element.8), channel_id=1, source_target_pairs={{1,0},{2,1},{3,2},{4,3},{5,4},{6,5},{7,6},{9,8},{10,9},{11,10},{12... | collective-permute-start | bytes 2211848 | tf_op jit(solution)/shard_map/ppermute | solution.py:15
  14.3 14.1 %copy-start.5 = (f32[128,16]{0,1:T(8,128)S(1)}, f32[128,16]{0,1:T(8,128)}, u32[]{:S(2)}) copy-start(f32[128,16]{0,1:T(8,128)} %param.12) | copy-start | bytes 24580
  14.3 14.1 %copy-start.4 = (f32[2,64,128]{2,1,0:T(8,128)S(1)}, f32[2,64,128]{2,1,0:T(8,128)}, u32[]{:S(2)}) copy-start(f32[2,64,128]{2,1,0:T(8,128)} %param.11) | copy-start | bytes 196612
  14.3 23.8 %copy-start.2 = (bf16[8,64,64]{2,1,0:T(8,128)(2,1)S(1)}, bf16[8,64,64]{2,1,0:T(8,128)(2,1)}, u32[]{:S(2)}) copy-start(bf16[8,64,64]{2,1,0:T(8,128)(2,1)} %param.9) | copy-start | bytes 196612
  14.3 23.8 %copy-start.6 = (f32[64]{0:T(128)S(1)}, f32[64]{0:T(128)}, u32[]{:S(2)}) copy-start(f32[64]{0:T(128)} %param.10) | copy-start | bytes 772
  15.7 22.4 %all-to-all-start = ((bf16[8,2,64,128]{3,1,0,2:T(2,128)(2,1)}), bf16[8,2,64,128]{3,1,0,2:T(2,128)(2,1)S(1)}, u32[]{:S(2)}, u32[]{:S(2)}) async-start(bf16[8,2,64,128]{3,1,0,2:T(2,128)(2,1)} %copy.17), calls=%async_computation | async-start | bytes 524288 | tf_op jit(solution)/shard_map/all_to_all | solution.py:52
  40.0 9.0 %all-to-all-start.1 = ((bf16[8,2,1024]{2,1,0:T(2,128)(2,1)}), bf16[8,2,1024]{2,1,0:T(2,128)(2,1)S(1)}, u32[]{:S(2)}, u32[]{:S(2)}) async-start(bf16[8,2,1024]{2,1,0:T(2,128)(2,1)} %reshape.22), calls=%async_computation.1 | async-start | bytes 65536 | tf_op jit(solution)/shard_map/all_to_all | solution.py:68
  49.8 11.7 %copy-start.3 = (bf16[16,8,720]{2,1,0:T(8,128)(2,1)S(1)}, bf16[16,8,720]{2,1,0:T(8,128)(2,1)}, u32[]{:S(2)}) copy-start(bf16[16,8,720]{2,1,0:T(8,128)(2,1)} %param.13) | copy-start | bytes 552964
